TPU v7x, 32 devices: a whole 2x2x4 slice. The times are simulated.
32 devices in a mesh: gx: 4 (over y, core), gy: 2 (over x), gz: 4 (over z).
Axes of the slice: x: 2, y: 2, z: 4, core: 2. Of those that a mesh axis runs over, the one named last changes fastest.
Arguments:
- positions: float32 [3, 4, 2, 4, 512], P(None, 'gx', 'gy', 'gz'), may hold values from 0 to 1
- velocities: float32 [3, 4, 2, 4, 512], P(None, 'gx', 'gy', 'gz'), may hold values from -6 to 6
- charges: float32 [4, 2, 4, 512], P('gx', 'gy', 'gz'), may hold values from -5 to 5
- cluster_atoms: int32 [4, 2, 4, 768], P('gx', 'gy', 'gz'), may hold values from 0 to 512, as said below
- pair_list: int32 [3, 4, 2, 4, 256], P(None, 'gx', 'gy', 'gz'), may hold values from 0 to 124, as said below
Outputs:
- new_positions: float32 [3, 4, 2, 4, 512], P(None, 'gx', 'gy', 'gz')
- new_velocities: float32 [3, 4, 2, 4, 512], P(None, 'gx', 'gy', 'gz')
- last_forces: float32 [3, 4, 2, 4, 512], P(None, 'gx', 'gy', 'gz')
Inputs may be any that keep to these rules, and one draw needn't show every extreme that they name: `cluster_atoms`: on every domain each atom index below 512 stands in exactly one slot; all other slots hold 512, meaning empty. `pair_list`: row 0 and row 1 lie in 0 to 5, row 2 in 0 to 124; on every domain each of the 125 shift indices appears in at least 2 listed pairs.
All inputs are finite; a program needn't handle non-finite values.
Results may differ from a plain program's by a relative error of at most 0.0001.
Values sent between devices are 32-bit elements; how exact they have to be, the bound alone decides.
A program may use at most 64 MiB of HBM per device.

v0:
```python
import jax
import jax.numpy as jnp
from jax import lax
from jax.sharding import PartitionSpec as P

CLUSTER = 128
A_DEV = 512
CL_DEV = 6
PAIRS_DEV = 256
STEPS = 2


CUTOFF_SQ = 4.0
SOFTENING = 0.5
TIME_STEP = 0.02
LEVEL_ORDER = (0, 3, 2, 1, 4)


def shifted(value, axis, by):
    count = lax.axis_size(axis)
    return lax.ppermute(value, axis, [(i, (i + by) % count) for i in range(count)])


def padded_2(block, sides, width):
    for axis, dim in sides:
        count = lax.axis_size(axis)
        forward = [(i, i + 1) for i in range(count - 1)]
        forward.append((count - 1, 0))
        backward = [(target, source) for source, target in forward]
        low = lax.ppermute(
            lax.slice_in_dim(block, block.shape[dim] - width, None, axis=dim), axis, forward
        )
        high = lax.ppermute(lax.slice_in_dim(block, 0, width, axis=dim), axis, backward)
        block = jnp.concatenate([low, block, high], axis=dim)
    return block


def pair_terms(left_xyz, left_charge, right_xyz, right_charge):
    separation = left_xyz[:, :, :, None] - right_xyz[:, :, None, :]
    distance_sq = jnp.sum(separation * separation, axis=0)
    window_term = jnp.maximum(1.0 - distance_sq / CUTOFF_SQ, 0.0)
    inverse = 1.0 / (distance_sq + SOFTENING)
    scalar = (
        2.0
        * left_charge[:, :, None]
        * right_charge[:, None, :]
        * (
            3.0 * window_term * window_term * inverse / CUTOFF_SQ
            + window_term * window_term * window_term * inverse * inverse
        )
    )
    pair_force = scalar[None] * separation
    return (jnp.sum(pair_force, axis=3), -jnp.sum(pair_force, axis=2))


def reverse_dims(values, dims):
    for dim_index in dims:
        values = jnp.flip(values, axis=dim_index)
    return values


def restore_order(values, dims):
    for dim_index in dims:
        values = jnp.take(values, jnp.array(LEVEL_ORDER, dtype=jnp.int32), axis=dim_index)
    return values


def move_along_x(values, stride):
    return shifted(values, "gx", stride)


def move_along_y(values, stride):
    return shifted(values, "gy", stride)


def move_along_z(values, stride):
    return shifted(values, "gz", stride)


def fold_levels(buffer, axis_dim, mover):
    layers = [
        lax.index_in_dim(buffer, level_index, axis_dim, keepdims=False) for level_index in range(5)
    ]
    summed = layers[2]
    for stride, outer_level, inner_level in ((1, 4, 3), (-1, 0, 1)):
        moving = layers[outer_level]
        for step_index in range(2):
            moving = mover(moving, stride)
            if step_index == 0:
                moving = moving + layers[inner_level]
        summed = summed + moving
    return summed


def fold_along_z(buffer, axis_dim):
    return fold_levels(buffer, axis_dim, move_along_z)


def shards(positions, velocities, charges, cluster_atoms, pair_list):
    slot_count = CL_DEV * CLUSTER
    block_pairs = 16
    blocks = PAIRS_DEV // block_pairs
    atom_slots = cluster_atoms.reshape(slot_count)
    charge_pad = jnp.concatenate([charges.reshape(A_DEV), jnp.zeros((1,), jnp.float32)])
    slot_charge = charge_pad[atom_slots]
    pairs = pair_list.reshape(3, PAIRS_DEV)
    shift_index = pairs[2]
    delta_x = shift_index // 25 - 2
    delta_y = shift_index // 5 % 5 - 2
    delta_z = shift_index % 5 - 2
    offsets = jnp.stack([delta_x, delta_y, delta_z]).astype(jnp.float32)
    zone_rows = shift_index * CL_DEV + pairs[1]
    home_rows = pairs[0]
    block_inputs = (
        home_rows.reshape(blocks, block_pairs),
        zone_rows.reshape(blocks, block_pairs),
        jnp.transpose(offsets.reshape(3, blocks, block_pairs), (1, 0, 2)),
    )
    coords = positions.reshape(3, A_DEV)
    velocity = velocities.reshape(3, A_DEV)
    forces = jnp.zeros_like(coords)
    for step_index in range(STEPS):
        padded = jnp.concatenate([coords, jnp.zeros((3, 1), jnp.float32)], axis=1)
        slot_xyz = padded[:, atom_slots]
        packed = jnp.concatenate([slot_xyz, slot_charge[None]], axis=0).reshape(
            4, 1, 1, 1, slot_count
        )
        near = padded_2(packed, (("gx", 1), ("gy", 2), ("gz", 3)), 1)
        far = padded_2(reverse_dims(near, (1, 2, 3)), (("gx", 1), ("gy", 2), ("gz", 3)), 1)
        zone_data = restore_order(far, (1, 2, 3))
        zone_data = zone_data.reshape(4, 125 * CL_DEV, CLUSTER)
        home_data = packed.reshape(4, CL_DEV, CLUSTER)

        def accumulate(carried, block_data):
            rows_left, rows_right, shift_vec = block_data
            left_xyz = home_data[:3][:, rows_left]
            right_xyz = zone_data[:3][:, rows_right] + shift_vec[:, :, None]
            left_force, right_force = pair_terms(
                left_xyz, home_data[3][rows_left], right_xyz, zone_data[3][rows_right]
            )
            return (
                (
                    carried[0].at[:, rows_left].add(left_force),
                    carried[1].at[:, rows_right].add(right_force),
                ),
                None,
            )

        start = (
            jnp.zeros((3, CL_DEV, CLUSTER), jnp.float32),
            jnp.zeros((3, 125 * CL_DEV, CLUSTER), jnp.float32),
        )
        (home_force, zone_force), _ = lax.scan(accumulate, start, block_inputs)
        zone_force = zone_force.reshape(3, 125, CL_DEV, CLUSTER).at[:, 62].add(home_force)
        zone_force = zone_force.reshape(3, 5, 5, 5, slot_count)
        folded = fold_levels(zone_force, 1, move_along_x)
        folded = fold_levels(folded, 1, move_along_y)
        folded = fold_along_z(folded, 1)
        forces = jnp.zeros((3, A_DEV + 1), jnp.float32).at[:, atom_slots].add(folded)[:, :A_DEV]
        velocity = velocity + TIME_STEP * forces
        coords = coords + TIME_STEP * velocity
    return (
        coords.reshape(positions.shape),
        velocity.reshape(positions.shape),
        forces.reshape(positions.shape),
    )


def solution(mesh):
    in_specs = (
        P(None, "gx", "gy", "gz", None),
        P(None, "gx", "gy", "gz", None),
        P("gx", "gy", "gz", None),
        P("gx", "gy", "gz", None),
        P(None, "gx", "gy", "gz", None),
    )
    out_specs = (
        P(None, "gx", "gy", "gz", None),
        P(None, "gx", "gy", "gz", None),
        P(None, "gx", "gy", "gz", None),
    )
    return jax.shard_map(shards, mesh=mesh, in_specs=in_specs, out_specs=out_specs, check_vma=False)
```

profile of v0, /device:TPU:0, one launch (start us, length us, event | category | flops | bytes accessed | tf_op | source)
XLA Modules:
  0.0 561.2 jit_solution(3806506472629168779)
XLA Ops:
  4.6 3.2 gather_fusion.9
  11.8 2.3 collective-permute-start.2
  22.3 3.6 collective-permute-done.4
  29.2 2.5 collective-permute-done.6
  33.9 5.5 collective-permute-done.8
  39.4 3.6 collective-permute-done.9
  44.3 2.7 collective-permute-start.11
  47.4 7.7 %collective-permute-done.10 = f32[4,5,5,1,768]{4,0,3,2,1:T(4,128)S(1)} collective-permute-done((f32[4,5,5,1,768]{4,0,3,2,1:T(4,128)S(1)}, f32[4,5,5,1,768]{4,0,3,2,1:T(4,128)S(1)}, u32[]{:S(2)}, u32[]{:S(2)}) %collective-permute-start.10) | collective-permute-done | bytes 307232 | tf_op jit(solution)/shard_map/ppermute | solution.py:30
  55.9 3.8 collective-permute-done.11
  70.6 162.0 %while.26 = (s32[]{:T(128)}, f32[3,6,128]{2,0,1:T(4,128)S(1)}, f32[3,750,128]{2,0,1:T(4,128)}, s32[16,16]{1,0:T(8,128)S(1)}, f32[4,6,128]{2,1,0:T(8,128)S(1)}, /...) while((s32[]{:T(128)}, f32[3,6,128]{2,0,1:T(4,128)S(1)}, ...), condition=%wide.region_6.10_spmd, body=%wide.region_0.0_spmd.sunk | while | flops 9453666 | bytes 8828709 | solution.py:153
  236.9 7.0 %collective-permute-done.12 = f32[3,5,5,768]{3,0,2,1:T(4,128)S(1)} collective-permute-done((f32[3,5,5,768]{3,0,2,1:T(4,128)S(1)}, f32[3,5,5,768]{3,0,2,1:T(4,128)S(1)}, u32[]{:S(2)}, u32[]{:S(2)}) %collective-permute-start.12) | collective-permute-done | bytes 230432 | tf_op jit(solution)/shard_map/ppermute | solution.py:21
  246.9 6.7 %collective-permute-done.13 = f32[3,5,5,768]{3,0,2,1:T(4,128)S(1)} collective-permute-done((f32[3,5,5,768]{3,0,2,1:T(4,128)S(1)}, f32[3,5,5,768]{3,0,2,1:T(4,128)S(1)}, u32[]{:S(2)}, u32[]{:S(2)}) %collective-permute-start.13) | collective-permute-done | bytes 230432 | tf_op jit(solution)/shard_map/ppermute | solution.py:21
  256.8 2.9 collective-permute-done.16
  263.1 2.6 collective-permute-done.17
  266.6 3.6 collective-permute-start.22
  272.4 3.5 collective-permute-start.23
  277.7 6.1 %scatter_custom_fusion.4 = f32[3,513]{0,1:T(8,128)S(1)} fusion(s32[768]{0:T(1024)S(1)} %fusion.63, f32[768,3]{1,0:T(8,128)S(1)} %copy.91, f32[]{:T(128)} %constant.175.clone.1), kind=kCustom, calls=%fused_computation.125 | custom fusion | flops 2304 | bytes 6160 | tf_op jit(solution)/shard_map/scatter-add | solution.py:159
  295.1 2.8 collective-permute-start.29
  297.9 3.8 collective-permute-done.28
  303.7 2.3 collective-permute-done.30
  308.5 5.0 collective-permute-done.32
  313.5 3.9 collective-permute-done.33
  321.6 8.0 %collective-permute-done.34 = f32[4,5,5,1,768]{4,0,3,2,1:T(4,128)S(1)} collective-permute-done((f32[4,5,5,1,768]{4,0,3,2,1:T(4,128)S(1)}, f32[4,5,5,1,768]{4,0,3,2,1:T(4,128)S(1)}, u32[]{:S(2)}, u32[]{:S(2)}) %collective-permute-start.34) | collective-permute-done | bytes 307232 | tf_op jit(solution)/shard_map/ppermute | solution.py:30
  330.3 4.8 collective-permute-done.35
  346.0 162.0 %while.27 = (s32[]{:T(128)}, f32[3,6,128]{2,0,1:T(4,128)S(1)}, f32[3,750,128]{2,0,1:T(4,128)}, s32[16,16]{1,0:T(8,128)S(1)}, f32[4,6,128]{2,1,0:T(8,128)S(1)}, /...) while((s32[]{:T(128)}, f32[3,6,128]{2,0,1:T(4,128)S(1)}, ...), condition=%wide.region_14.18_spmd, body=%wide.region_8.17_spmd.sunk | while | flops 9453666 | bytes 8828709 | solution.py:153
  512.3 6.4 %collective-permute-done.36 = f32[3,5,5,768]{3,0,2,1:T(4,128)S(1)} collective-permute-done((f32[3,5,5,768]{3,0,2,1:T(4,128)S(1)}, f32[3,5,5,768]{3,0,2,1:T(4,128)S(1)}, u32[]{:S(2)}, u32[]{:S(2)}) %collective-permute-start.36) | collective-permute-done | bytes 230432 | tf_op jit(solution)/shard_map/ppermute | solution.py:21
  522.0 6.3 %collective-permute-done.37 = f32[3,5,5,768]{3,0,2,1:T(4,128)S(1)} collective-permute-done((f32[3,5,5,768]{3,0,2,1:T(4,128)S(1)}, f32[3,5,5,768]{3,0,2,1:T(4,128)S(1)}, u32[]{:S(2)}, u32[]{:S(2)}) %collective-permute-start.37) | collective-permute-done | bytes 230432 | tf_op jit(solution)/shard_map/ppermute | solution.py:21
  531.6 2.6 collective-permute-done.40
  537.9 2.8 collective-permute-done.41
  542.2 3.2 collective-permute-start.46
  547.2 4.1 collective-permute-start.47
  552.9 6.1 %scatter_custom_fusion.5 = f32[3,513]{0,1:T(8,128)S(1)} fusion(s32[768]{0:T(1024)S(1)} %fusion.63, f32[768,3]{1,0:T(8,128)S(1)} %copy.96, f32[]{:T(128)} %constant.175.clone.1), kind=kCustom, calls=%fused_computation.123 | custom fusion | flops 2304 | bytes 6160 | tf_op jit(solution)/shard_map/scatter-add | solution.py:159
  (979 shorter events, 425.6 us)
Async XLA Ops:
  18.1 7.8 %collective-permute-start.4 = (f32[4,3,3,1,768]{4,0,3,2,1:T(4,128)S(1)}, f32[4,3,3,1,768]{4,0,3,2,1:T(4,128)S(1)}, u32[]{:S(2)}, u32[]{:S(2)}) collective-permute-start(f32[4,3,3,1,768]{4,0,3,2,1:T(4,128)S(1)} %pad_maximum_fusion.20), channel_id=1, source_target_pairs={{0,1},{1,2},{2,3},{3,0},{4,5},{5,6},{6,7},{7,4},{8,9},{9,10},{10,1... | collective-permute-start | bytes 331784 | tf_op jit(solution)/shard_map/ppermute | solution.py:30
  19.8 7.2 %collective-permute-start.5 = (f32[4,3,3,1,768]{4,0,3,2,1:T(4,128)S(1)}, f32[4,3,3,1,768]{4,0,3,2,1:T(4,128)S(1)}, u32[]{:S(2)}, u32[]{:S(2)}) collective-permute-start(f32[4,3,3,1,768]{4,0,3,2,1:T(4,128)S(1)} %pad_maximum_fusion.20), channel_id=1, source_target_pairs={{1,0},{2,1},{3,2},{0,3},{5,4},{6,5},{7,6},{4,7},{9,8},{10,9},{11,1... | collective-permute-start | bytes 331784 | tf_op jit(solution)/shard_map/ppermute | solution.py:33
  31.8 7.6 %collective-permute-start.8 = (f32[4,5,1,3,768]{4,0,3,2,1:T(4,128)S(1)}, f32[4,5,1,3,768]{4,0,3,2,1:T(4,128)S(1)}, u32[]{:S(2)}, u32[]{:S(2)}) collective-permute-start(f32[4,5,1,3,768]{4,0,3,2,1:T(4,128)S(1)} %get-tuple-element.243), channel_id=1, source_target_pairs={{0,4},{4,0},{1,5},{5,1},{2,6},{6,2},{3,7},{7,3},{8,12},{12,8},{9,1... | collective-permute-start | bytes 552968 | tf_op jit(solution)/shard_map/ppermute | solution.py:30
  32.4 10.6 %collective-permute-start.9 = (f32[4,5,1,3,768]{4,0,3,2,1:T(4,128)S(1)}, f32[4,5,1,3,768]{4,0,3,2,1:T(4,128)S(1)}, u32[]{:S(2)}, u32[]{:S(2)}) collective-permute-start(f32[4,5,1,3,768]{4,0,3,2,1:T(4,128)S(1)} %get-tuple-element.244), channel_id=1, source_target_pairs={{4,0},{0,4},{5,1},{1,5},{6,2},{2,6},{7,3},{3,7},{12,8},{8,12},{13,... | collective-permute-start | bytes 552968 | tf_op jit(solution)/shard_map/ppermute | solution.py:33
  43.1 12.0 %collective-permute-start.10 = (f32[4,5,5,1,768]{4,0,3,2,1:T(4,128)S(1)}, f32[4,5,5,1,768]{4,0,3,2,1:T(4,128)S(1)}, u32[]{:S(2)}, u32[]{:S(2)}) collective-permute-start(f32[4,5,5,1,768]{4,0,3,2,1:T(4,128)S(1)} %get-tuple-element.237), channel_id=1, source_target_pairs={{0,1},{1,2},{2,3},{3,0},{4,5},{5,6},{6,7},{7,4},{8,9},{9,10},{10,1... | collective-permute-start | bytes 921608 | tf_op jit(solution)/shard_map/ppermute | solution.py:30
  44.3 15.4 %collective-permute-start.11 = (f32[4,5,5,1,768]{4,0,3,2,1:T(4,128)S(1)}, f32[4,5,5,1,768]{4,0,3,2,1:T(4,128)}, u32[]{:S(2)}, u32[]{:S(2)}) collective-permute-start(f32[4,5,5,1,768]{4,0,3,2,1:T(4,128)S(1)} %get-tuple-element.238), channel_id=1, source_target_pairs={{1,0},{2,1},{3,2},{0,3},{5,4},{6,5},{7,6},{4,7},{9,8},{10,9},{11,1... | collective-permute-start | bytes 921608 | tf_op jit(solution)/shard_map/ppermute | solution.py:33
  235.1 8.8 %collective-permute-start.12 = (f32[3,5,5,768]{3,0,2,1:T(4,128)S(1)}, f32[3,5,5,768]{3,0,2,1:T(4,128)S(1)}, u32[]{:S(2)}, u32[]{:S(2)}) collective-permute-start(f32[3,5,5,768]{3,0,2,1:T(4,128)S(1)} %get-tuple-element.233), channel_id=1, source_target_pairs={{0,8},{8,16},{16,24},{24,0},{1,9},{9,17},{17,25},{25,1},{2,10},{10... | collective-permute-start | bytes 691208 | tf_op jit(solution)/shard_map/ppermute | solution.py:21
  235.1 8.7 %collective-permute-start.14 = (f32[3,5,5,768]{3,0,2,1:T(4,128)S(1)}, f32[3,5,5,768]{3,0,2,1:T(4,128)S(1)}, u32[]{:S(2)}, u32[]{:S(2)}) collective-permute-start(f32[3,5,5,768]{3,0,2,1:T(4,128)S(1)} %get-tuple-element.234), channel_id=1, source_target_pairs={{0,24},{8,0},{16,8},{24,16},{1,25},{9,1},{17,9},{25,17},{2,26},{10... | collective-permute-start | bytes 691208 | tf_op jit(solution)/shard_map/ppermute | solution.py:21
  245.1 8.5 %collective-permute-start.13 = (f32[3,5,5,768]{3,0,2,1:T(4,128)S(1)}, f32[3,5,5,768]{3,0,2,1:T(4,128)S(1)}, u32[]{:S(2)}, u32[]{:S(2)}) collective-permute-start(f32[3,5,5,768]{3,0,2,1:T(4,128)S(1)} %get-tuple-element.231), channel_id=1, source_target_pairs={{0,8},{8,16},{16,24},{24,0},{1,9},{9,17},{17,25},{25,1},{2,10},{10... | collective-permute-start | bytes 691208 | tf_op jit(solution)/shard_map/ppermute | solution.py:21
  245.8 7.8 %collective-permute-start.15 = (f32[3,5,5,768]{3,0,2,1:T(4,128)S(1)}, f32[3,5,5,768]{3,0,2,1:T(4,128)S(1)}, u32[]{:S(2)}, u32[]{:S(2)}) collective-permute-start(f32[3,5,5,768]{3,0,2,1:T(4,128)S(1)} %get-tuple-element.232), channel_id=1, source_target_pairs={{0,24},{8,0},{16,8},{24,16},{1,25},{9,1},{17,9},{25,17},{2,26},{10... | collective-permute-start | bytes 691208 | tf_op jit(solution)/shard_map/ppermute | solution.py:21
  254.7 4.9 collective-permute-start.16
  255.1 5.8 %collective-permute-start.18 = (f32[3,5,768]{2,0,1:T(4,128)S(1)}, f32[3,5,768]{2,0,1:T(4,128)S(1)}, u32[]{:S(2)}, u32[]{:S(2)}) collective-permute-start(f32[3,5,768]{2,0,1:T(4,128)S(1)} %get-tuple-element.256), channel_id=1, source_target_pairs={{0,4},{4,0},{1,5},{5,1},{2,6},{6,2},{3,7},{7,3},{8,12},{12,8},{9,1... | collective-permute-start | bytes 138248 | tf_op jit(solution)/shard_map/ppermute | solution.py:21
  261.5 4.9 collective-permute-start.19
  266.4 5.5 collective-permute-start.20
  266.6 5.3 collective-permute-start.22
  272.0 5.5 collective-permute-start.21
  272.4 5.1 collective-permute-start.23
  293.9 7.8 %collective-permute-start.28 = (f32[4,3,3,1,768]{4,0,3,2,1:T(4,128)S(1)}, f32[4,3,3,1,768]{4,0,3,2,1:T(4,128)S(1)}, u32[]{:S(2)}, u32[]{:S(2)}) collective-permute-start(f32[4,3,3,1,768]{4,0,3,2,1:T(4,128)S(1)} %pad_maximum_fusion.21), channel_id=1, source_target_pairs={{0,1},{1,2},{2,3},{3,0},{4,5},{5,6},{6,7},{7,4},{8,9},{9,10},{10,1... | collective-permute-start | bytes 331784 | tf_op jit(solution)/shard_map/ppermute | solution.py:30
  295.1 6.6 %collective-permute-start.29 = (f32[4,3,3,1,768]{4,0,3,2,1:T(4,128)S(1)}, f32[4,3,3,1,768]{4,0,3,2,1:T(4,128)S(1)}, u32[]{:S(2)}, u32[]{:S(2)}) collective-permute-start(f32[4,3,3,1,768]{4,0,3,2,1:T(4,128)S(1)} %pad_maximum_fusion.21), channel_id=1, source_target_pairs={{1,0},{2,1},{3,2},{0,3},{5,4},{6,5},{7,6},{4,7},{9,8},{10,9},{11,1... | collective-permute-start | bytes 331784 | tf_op jit(solution)/shard_map/ppermute | solution.py:33
  306.4 7.1 %collective-permute-start.32 = (f32[4,5,1,3,768]{4,0,3,2,1:T(4,128)S(1)}, f32[4,5,1,3,768]{4,0,3,2,1:T(4,128)S(1)}, u32[]{:S(2)}, u32[]{:S(2)}) collective-permute-start(f32[4,5,1,3,768]{4,0,3,2,1:T(4,128)S(1)} %get-tuple-element.241), channel_id=1, source_target_pairs={{0,4},{4,0},{1,5},{5,1},{2,6},{6,2},{3,7},{7,3},{8,12},{12,8},{9,1... | collective-permute-start | bytes 552968 | tf_op jit(solution)/shard_map/ppermute | solution.py:30
  307.4 10.0 %collective-permute-start.33 = (f32[4,5,1,3,768]{4,0,3,2,1:T(4,128)S(1)}, f32[4,5,1,3,768]{4,0,3,2,1:T(4,128)S(1)}, u32[]{:S(2)}, u32[]{:S(2)}) collective-permute-start(f32[4,5,1,3,768]{4,0,3,2,1:T(4,128)S(1)} %get-tuple-element.242), channel_id=1, source_target_pairs={{4,0},{0,4},{5,1},{1,5},{6,2},{2,6},{7,3},{3,7},{12,8},{8,12},{13,... | collective-permute-start | bytes 552968 | tf_op jit(solution)/shard_map/ppermute | solution.py:33
  317.5 12.0 %collective-permute-start.34 = (f32[4,5,5,1,768]{4,0,3,2,1:T(4,128)S(1)}, f32[4,5,5,1,768]{4,0,3,2,1:T(4,128)S(1)}, u32[]{:S(2)}, u32[]{:S(2)}) collective-permute-start(f32[4,5,5,1,768]{4,0,3,2,1:T(4,128)S(1)} %get-tuple-element.235), channel_id=1, source_target_pairs={{0,1},{1,2},{2,3},{3,0},{4,5},{5,6},{6,7},{7,4},{8,9},{9,10},{10,1... | collective-permute-start | bytes 921608 | tf_op jit(solution)/shard_map/ppermute | solution.py:30
  319.2 15.9 %collective-permute-start.35 = (f32[4,5,5,1,768]{4,0,3,2,1:T(4,128)S(1)}, f32[4,5,5,1,768]{4,0,3,2,1:T(4,128)}, u32[]{:S(2)}, u32[]{:S(2)}) collective-permute-start(f32[4,5,5,1,768]{4,0,3,2,1:T(4,128)S(1)} %get-tuple-element.236), channel_id=1, source_target_pairs={{1,0},{2,1},{3,2},{0,3},{5,4},{6,5},{7,6},{4,7},{9,8},{10,9},{11,1... | collective-permute-start | bytes 921608 | tf_op jit(solution)/shard_map/ppermute | solution.py:33
  510.5 8.2 %collective-permute-start.36 = (f32[3,5,5,768]{3,0,2,1:T(4,128)S(1)}, f32[3,5,5,768]{3,0,2,1:T(4,128)S(1)}, u32[]{:S(2)}, u32[]{:S(2)}) collective-permute-start(f32[3,5,5,768]{3,0,2,1:T(4,128)S(1)} %get-tuple-element.229), channel_id=1, source_target_pairs={{0,8},{8,16},{16,24},{24,0},{1,9},{9,17},{17,25},{25,1},{2,10},{10... | collective-permute-start | bytes 691208 | tf_op jit(solution)/shard_map/ppermute | solution.py:21
  510.5 8.2 %collective-permute-start.38 = (f32[3,5,5,768]{3,0,2,1:T(4,128)S(1)}, f32[3,5,5,768]{3,0,2,1:T(4,128)S(1)}, u32[]{:S(2)}, u32[]{:S(2)}) collective-permute-start(f32[3,5,5,768]{3,0,2,1:T(4,128)S(1)} %get-tuple-element.230), channel_id=1, source_target_pairs={{0,24},{8,0},{16,8},{24,16},{1,25},{9,1},{17,9},{25,17},{2,26},{10... | collective-permute-start | bytes 691208 | tf_op jit(solution)/shard_map/ppermute | solution.py:21
  520.0 8.4 %collective-permute-start.37 = (f32[3,5,5,768]{3,0,2,1:T(4,128)S(1)}, f32[3,5,5,768]{3,0,2,1:T(4,128)S(1)}, u32[]{:S(2)}, u32[]{:S(2)}) collective-permute-start(f32[3,5,5,768]{3,0,2,1:T(4,128)S(1)} %get-tuple-element.227), channel_id=1, source_target_pairs={{0,8},{8,16},{16,24},{24,0},{1,9},{9,17},{17,25},{25,1},{2,10},{10... | collective-permute-start | bytes 691208 | tf_op jit(solution)/shard_map/ppermute | solution.py:21
  521.2 7.2 %collective-permute-start.39 = (f32[3,5,5,768]{3,0,2,1:T(4,128)S(1)}, f32[3,5,5,768]{3,0,2,1:T(4,128)S(1)}, u32[]{:S(2)}, u32[]{:S(2)}) collective-permute-start(f32[3,5,5,768]{3,0,2,1:T(4,128)S(1)} %get-tuple-element.228), channel_id=1, source_target_pairs={{0,24},{8,0},{16,8},{24,16},{1,25},{9,1},{17,9},{25,17},{2,26},{10... | collective-permute-start | bytes 691208 | tf_op jit(solution)/shard_map/ppermute | solution.py:21
  535.8 4.9 collective-permute-start.41
  541.5 5.5 collective-permute-start.44
  542.2 4.9 collective-permute-start.46
  547.1 5.5 collective-permute-start.45
  547.2 5.5 collective-permute-start.47
  (25 other events, 247.6 us)
where the time goes:
time: 563 us; the launch traced here: 561 us
  other arithmetic  246 us (44%)
  local copies, waits for them, and re-layouts  132 us (23%)
  waiting for transfers between devices  113 us (20%)
  starting transfers between devices  63.8 us (11%)
    scatter-add x32, other arithmetic, accumulate(): carried[1].at[:, rows_right].add(right_force)  67.3 us
    reduce_sum x32, other arithmetic, pair_terms(): return (jnp.sum(pair_force, axis=3), -jnp.sum(pair_force, axis=2))  63.4 us
    ppermute x24, waiting for transfers between devices, shifted(): lax.ppermute(value, axis, [(i, (i + by) % count) for i in range(count)])  47.9 us
    ppermute x12, waiting for transfers between devices, padded_2(): lax.ppermute(lax.slice_in_dim(block, block.shape[dim] - width, None, axis...  45 us
    scatter-add x32, other arithmetic, accumulate(): carried[0].at[:, rows_left].add(left_force)  35.7 us
    reduce_sum x32, other arithmetic, pair_terms(): distance_sq = jnp.sum(separation * separation, axis=0)  33.3 us
    ppermute x24, starting transfers between devices, shifted(): lax.ppermute(value, axis, [(i, (i + by) % count) for i in range(count)])  31.6 us
    another operation x68, local copies, waits for them, and re-layouts  21.9 us
  transfers between devices with their start and end apart: 48, of which 39 were waited for; matrix products, arithmetic and copies ran while one was open for 0% of the time, Pallas kernels for 0%

commit v1 on v0

v1 whole, which is shorter than its diff:
```python
import functools

import jax
import jax.numpy as jnp
from jax import lax
from jax.experimental import pallas as pl
from jax.experimental.pallas import tpu as pltpu
from jax.sharding import PartitionSpec as P

CLUSTER = 128
STEPS = 2
TIME_STEP = 0.02
MESH = pl.DeviceIdType.MESH
AXES = ("gx", "gy", "gz")
VMEM = pl.BlockSpec(memory_space=pltpu.VMEM)
SMEM = pl.BlockSpec(memory_space=pltpu.SMEM)
UNROLL = 4


def split3(value):
    hi = value.astype(jnp.bfloat16)
    rest = value - hi.astype(jnp.float32)
    mid = rest.astype(jnp.bfloat16)
    lo = (rest - mid.astype(jnp.float32)).astype(jnp.bfloat16)
    return hi, mid, lo


class Zone:
    def __init__(self, sizes):
        self.sizes = sizes
        self.spans = tuple(min(5, n) for n in sizes)
        self.lows = tuple(-2 if n >= 5 else 0 for n in sizes)
        self.count = self.spans[0] * self.spans[1] * self.spans[2]
        own = tuple(-low for low in self.lows)
        self.own = (own[0] * self.spans[1] + own[1]) * self.spans[2] + own[2]

    def place(self, deltas):
        index = 0
        for delta, n, span in zip(deltas, self.sizes, self.spans):
            if n >= 5:
                here = delta + 2
            elif n in (1, 2, 4):
                here = (delta + 2 * n) & (n - 1)
            else:
                here = lax.rem(delta + 2 * n, n)
            index = index * span + here
        return index

    def peer(self, index, sign):
        parts = (
            index // (self.spans[1] * self.spans[2]),
            (index // self.spans[2]) % self.spans[1],
            index % self.spans[2],
        )
        out = []
        for axis, n, low, part in zip(AXES, self.sizes, self.lows, parts):
            out.append((lax.axis_index(axis) + sign * (part + low) + 2 * n) % n)
        return tuple(out)

    def others(self, body):
        def step(k, carry):
            body((self.own + 1 + k) % self.count)
            return carry

        lax.fori_loop(0, self.count - 1, step, 0)


def enter(zone):
    barrier = pltpu.get_barrier_semaphore()

    def greet(index):
        pl.semaphore_signal(barrier, 1, device_id=zone.peer(index, 1), device_id_type=MESH)

    zone.others(greet)
    pl.semaphore_wait(barrier, zone.count - 1)


def one_hot(atoms_ref, atom_count):
    slots = atoms_ref.shape[1]
    rows = lax.broadcasted_iota(jnp.int32, (atom_count, slots), 0)
    return jnp.where(rows == atoms_ref[...], 1.0, 0.0).astype(jnp.bfloat16)


def spread_kernel(zone, rows, x_ref, v_ref, q_ref, atoms_ref, zone_ref, vel_ref, send_sem, recv_sem):
    atom_count = x_ref.shape[1]
    clusters = atoms_ref.shape[1] // CLUSTER
    data = jnp.concatenate(
        [x_ref[...], v_ref[...], q_ref[...], jnp.zeros((1, atom_count), jnp.float32)], axis=0
    )
    hi, mid, lo = split3(data)
    stacked = jnp.concatenate([hi, mid, lo, jnp.zeros_like(hi)], axis=0)
    out = jnp.dot(stacked, one_hot(atoms_ref, atom_count), preferred_element_type=jnp.float32)
    slot = out[0:8] + out[8:16] + out[16:24]
    for k in range(clusters):
        lanes = slice(k * CLUSTER, (k + 1) * CLUSTER)
        for c in range(3):
            zone_ref[zone.own, c * clusters + k, :] = slot[c, lanes]
            vel_ref[c * clusters + k, :] = slot[3 + c, lanes]
        zone_ref[zone.own, 3 * clusters + k, :] = slot[6, lanes]
    enter(zone)
    share(zone, zone_ref, send_sem, recv_sem, 4 * clusters)


def share(zone, zone_ref, send_sem, recv_sem, rows):
    def copy(index):
        return pltpu.make_async_remote_copy(
            src_ref=zone_ref.at[zone.own, pl.ds(0, rows)],
            dst_ref=zone_ref.at[index, pl.ds(0, rows)],
            send_sem=send_sem.at[index],
            recv_sem=recv_sem.at[index],
            device_id=zone.peer(index, -1),
            device_id_type=MESH,
        )

    zone.others(lambda index: copy(index).start())
    zone.others(lambda index: copy(index).wait())


def gathered_force(zone, force_ref, land_ref, send_sem, recv_sem):
    def copy(index):
        return pltpu.make_async_remote_copy(
            src_ref=force_ref.at[index],
            dst_ref=land_ref.at[index],
            send_sem=send_sem.at[index],
            recv_sem=recv_sem.at[index],
            device_id=zone.peer(index, 1),
            device_id_type=MESH,
        )

    zone.others(lambda index: copy(index).start())
    zone.others(lambda index: copy(index).wait())

    def add(k, total):
        return total + land_ref[(zone.own + 1 + k) % zone.count]

    return lax.fori_loop(0, zone.count - 1, add, force_ref[zone.own])


def advance_kernel(
    zone, rows, force_ref, x_ref, vel_ref, zone_ref, new_vel_ref,
    land_ref, send_sem, recv_sem, send_sem2, recv_sem2,
):
    enter(zone)
    force = gathered_force(zone, force_ref, land_ref, send_sem, recv_sem)
    velocity = vel_ref[...] + TIME_STEP * force
    zone_ref[zone.own, pl.ds(0, rows)] = x_ref[...] + TIME_STEP * velocity
    new_vel_ref[...] = velocity
    share(zone, zone_ref, send_sem2, recv_sem2, rows)


def finish_kernel(
    zone, rows, force_ref, x_ref, vel_ref, atoms_ref, x_out, v_out, f_out,
    land_ref, slot_ref, send_sem, recv_sem,
):
    slots = atoms_ref.shape[1]
    clusters = slots // CLUSTER
    atom_count = x_out.shape[1]
    enter(zone)
    force = gathered_force(zone, force_ref, land_ref, send_sem, recv_sem)
    velocity = vel_ref[...] + TIME_STEP * force
    coords = x_ref[...] + TIME_STEP * velocity
    slot_ref[...] = jnp.zeros_like(slot_ref)
    for k in range(clusters):
        lanes = slice(k * CLUSTER, (k + 1) * CLUSTER)
        for c in range(3):
            r = c * clusters + k
            slot_ref[pl.ds(c, 1), lanes] = coords[r : r + 1]
            slot_ref[pl.ds(3 + c, 1), lanes] = velocity[r : r + 1]
            slot_ref[pl.ds(6 + c, 1), lanes] = force[r : r + 1]
    stacked = jnp.concatenate(split3(slot_ref[...]), axis=0)
    out = lax.dot_general(
        stacked, one_hot(atoms_ref, atom_count), (((1,), (1,)), ((), ())),
        preferred_element_type=jnp.float32,
    )
    atom = out[0:16] + out[16:32] + out[32:48]
    x_out[...] = atom[0:3]
    v_out[...] = atom[3:6]
    f_out[...] = atom[6:9]


def weighted(coords, charge):
    charge = 0.125 * charge
    part = jnp.concatenate([charge * c for c in coords] + [charge], axis=0)
    pieces = [p.astype(jnp.float32) for p in split3(part)]
    stacked = jnp.concatenate(pieces + [jnp.zeros_like(part)], axis=0).astype(jnp.bfloat16)
    return jnp.concatenate([stacked, stacked], axis=1)


def folded(out):
    return out[0:4] + out[4:8] + out[8:12]


def pair_kernel(zone, clusters, pairs_ref, x_ref, q_ref, force_ref, left_ref, lw_ref, acc_ref):
    own = zone.own
    for k in range(clusters):
        coords = []
        for c in range(3):
            row = x_ref[own, pl.ds(c * clusters + k, 1), :]
            coords.append(row)
            left_ref[k, c] = jnp.transpose(jnp.broadcast_to(0.5 * row, (CLUSTER, CLUSTER)))
        lw_ref[k] = weighted(coords, q_ref[own, pl.ds(3 * clusters + k, 1), :])
    acc_ref[...] = jnp.zeros_like(acc_ref)
    force_ref[...] = jnp.zeros_like(force_ref)

    def one(p):
        i = pairs_ref[0, p]
        j = pairs_ref[1, p]
        t = pairs_ref[2, p]
        t25 = (t * 5243) >> 17
        t5 = (t * 205) >> 10
        deltas = (t25 - 2, t5 - 5 * t25 - 2, t - 5 * t5 - 2)
        z = zone.place(deltas)
        coords = [
            x_ref[z, pl.ds(c * clusters + j, 1), :] + deltas[c].astype(jnp.float32)
            for c in range(3)
        ]
        charge = q_ref[z, pl.ds(3 * clusters + j, 1), :]
        r2 = None
        for c in range(3):
            d = left_ref[i, c] - 0.5 * coords[c]
            r2 = d * d if r2 is None else r2 + d * d
        g = jnp.maximum(1.0 - r2, 0.0)
        t = g * (1.0 / (r2 + 0.125))
        f = (g * t) * (t + 3.0)
        hi = f.astype(jnp.bfloat16)
        lo = (f - hi.astype(jnp.float32)).astype(jnp.bfloat16)
        out_left = lax.dot_general(
            weighted(coords, charge), jnp.concatenate([hi, lo], axis=1),
            (((1,), (1,)), ((), ())), preferred_element_type=jnp.float32,
        )
        out_right = jnp.dot(
            lw_ref[i], jnp.concatenate([hi, lo], axis=0), preferred_element_type=jnp.float32
        )
        return i, j, z, coords, charge, out_left, out_right

    def block(b, carry):
        done = [one(b * UNROLL + n) for n in range(UNROLL)]
        for i, j, z, coords, charge, out_left, out_right in done:
            acc_ref[i] += out_left
            sums = folded(out_right)
            for c in range(3):
                row = pl.ds(c * clusters + j, 1)
                force_ref[z, row, :] += charge * (coords[c] * sums[3:4] - sums[c : c + 1])
        return carry

    lax.fori_loop(0, pairs_ref.shape[1] // UNROLL, block, 0)
    for k in range(clusters):
        sums = folded(acc_ref[k])
        charge = q_ref[own, pl.ds(3 * clusters + k, 1), :]
        for c in range(3):
            row = pl.ds(c * clusters + k, 1)
            force_ref[own, row, :] += charge * (x_ref[own, row, :] * sums[3:4] - sums[c : c + 1])


def shards(sizes, positions, velocities, charges, cluster_atoms, pair_list):
    zone = Zone(sizes)
    atom_count = positions.shape[-1]
    slots = cluster_atoms.shape[-1]
    clusters = slots // CLUSTER
    rows = 3 * clusters
    f32 = jnp.float32
    x = positions.reshape(3, atom_count)
    v = velocities.reshape(3, atom_count)
    q = charges.reshape(1, atom_count)
    atoms = cluster_atoms.reshape(1, slots)
    pairs = pair_list.reshape(3, pair_list.shape[-1])
    sems = [pltpu.SemaphoreType.DMA((zone.count,))] * 2
    land = pltpu.VMEM((zone.count, rows, CLUSTER), f32)

    def params(number):
        return pltpu.CompilerParams(collective_id=number, has_side_effects=True)

    zone_shape = jax.ShapeDtypeStruct((zone.count, 4 * clusters, CLUSTER), f32)
    vel_shape = jax.ShapeDtypeStruct((rows, CLUSTER), f32)
    zone_x, vel = pl.pallas_call(
        functools.partial(spread_kernel, zone, rows),
        out_shape=(zone_shape, vel_shape),
        in_specs=[VMEM] * 4,
        out_specs=(VMEM, VMEM),
        scratch_shapes=sems,
        compiler_params=params(0),
        name="spread",
    )(x, v, q, atoms)
    zone_q = zone_x
    pair_call = pl.pallas_call(
        functools.partial(pair_kernel, zone, clusters),
        out_shape=jax.ShapeDtypeStruct((zone.count, rows, CLUSTER), f32),
        in_specs=[SMEM, VMEM, VMEM],
        out_specs=VMEM,
        scratch_shapes=[
            pltpu.VMEM((clusters, 3, CLUSTER, CLUSTER), f32),
            pltpu.VMEM((clusters, 16, 2 * CLUSTER), jnp.bfloat16),
            pltpu.VMEM((clusters, 16, CLUSTER), f32),
        ],
        name="pairs",
    )
    for step in range(STEPS):
        force = pair_call(pairs, zone_x, zone_q)
        own_x = zone_x[zone.own, :rows]
        if step < STEPS - 1:
            zone_x, vel = pl.pallas_call(
                functools.partial(advance_kernel, zone, rows),
                out_shape=(zone_shape, vel_shape),
                in_specs=[VMEM] * 3,
                out_specs=(VMEM, VMEM),
                scratch_shapes=[land] + sems + sems,
                compiler_params=params(1 + step),
                name="advance",
            )(force, own_x, vel)
        else:
            shape = jax.ShapeDtypeStruct((3, atom_count), f32)
            outs = pl.pallas_call(
                functools.partial(finish_kernel, zone, rows),
                out_shape=(shape, shape, shape),
                in_specs=[VMEM] * 4,
                out_specs=(VMEM, VMEM, VMEM),
                scratch_shapes=[land, pltpu.VMEM((16, slots), f32)] + sems,
                compiler_params=params(1 + step),
                name="finish",
            )(force, own_x, vel, atoms)
    return tuple(out.reshape(positions.shape) for out in outs)


def solution(mesh):
    spec3 = P(None, "gx", "gy", "gz", None)
    spec1 = P("gx", "gy", "gz", None)
    sizes = tuple(mesh.shape[axis] for axis in AXES)
    return jax.shard_map(
        functools.partial(shards, sizes),
        mesh=mesh,
        in_specs=(spec3, spec3, spec1, spec1, spec3),
        out_specs=(spec3, spec3, spec3),
        check_vma=False,
    )
```

time: 563 us -> 114 us (0.20)
  other arithmetic: 246 us -> 0 us
  local copies, waits for them, and re-layouts: 132 us -> 7.1 us
  waiting for transfers between devices: 113 us -> 0 us
  Pallas kernels: 0 us -> 106 us
  starting transfers between devices: 63.8 us -> 0 us
    scatter-add x68 -> x0, other arithmetic: 118 us -> none  [the longest x32 67.3 us: accumulate(): carried[1].at[:, rows_right].add(right_force)]
    ppermute x48 -> x0, waiting for transfers between devices: 113 us -> none  [the longest x24 47.9 us: shifted(): lax.ppermute(value, axis, [(i, (i + by) % count) for i in range(count)])]
    pallas_call x0 -> x5, Pallas kernels: none -> 106 us  [the longest x2 45.4 us: shards(): force = pair_call(pairs, zone_x, zone_q)]
    reduce_sum x64 -> x0, other arithmetic: 96.7 us -> none  [the longest x32 63.4 us: pair_terms(): return (jnp.sum(pair_force, axis=3), -jnp.sum(pair_force, axis=2))]
    gather x173 -> x0, local copies, waits for them, and re-layouts: 93 us -> none  [the longest x64 19 us: accumulate(): left_xyz = home_data[:3][:, rows_left]]
    ppermute x48 -> x0, starting transfers between devices: 63.8 us -> none  [the longest x24 31.6 us: shifted(): lax.ppermute(value, axis, [(i, (i + by) % count) for i in range(count)])]
    another operation x69 -> x0, local copies, waits for them, and re-layouts: 22 us -> none
    mul x64 -> x0, other arithmetic: 18.2 us -> none  [pair_terms(): 2.0 * left_charge[:, :, None] * right_charge[:, None, :]]
  transfers between devices with their start and end apart: 48 -> 0, of which waited for: 39 -> 0; matrix products, arithmetic and copies ran while one was open for 0% -> 0% of each run, Pallas kernels for 0% -> 0%
where the time goes in v1:
time: 114 us
  Pallas kernels  106 us (93%)
  local copies, waits for them, and re-layouts  7.1 us (6%)
    pallas_call x2, Pallas kernels, shards(): force = pair_call(pairs, zone_x, zone_q)  45.4 us
    pallas_call x1, Pallas kernels, shards(): pl.pallas_call(functools.partial(advance_kernel, zone, rows), out_shape=(...  25.5 us
    pallas_call x1, Pallas kernels, shards(): pl.pallas_call(functools.partial(spread_kernel, zone, rows), out_shape=(z...  20.3 us
    pallas_call x1, Pallas kernels, shards(): pl.pallas_call(functools.partial(finish_kernel, zone, rows), out_shape=(s...  14.6 us
    unnamed x15, local copies, waits for them, and re-layouts  4.49 us
    squeeze x2, local copies, waits for them, and re-layouts, shards(): own_x = zone_x[zone.own, :rows]  2.61 us

profile of v1, /device:TPU:0, one launch (start us, length us, event | category | flops | bytes accessed | tf_op | source)
XLA Modules:
  0.0 113.6 jit_solution(12991787856029725452)
XLA Ops:
  0.6 0.0 copy-start.3
  0.6 0.0 copy-start.4
  0.7 1.3 %copy.17 = s32[3,1,1,1,256]{4,0,2,1,3:T(4,128)} copy(s32[3,1,1,1,256]{4,3,2,1,0:T(1,128)} %param.9) | data formatting | bytes 6144
  1.9 0.0 copy-done.3
  1.9 0.0 copy-done.4
  1.9 0.6 copy_bitcast_fusion
  2.5 20.3 %spread.1 = (f32[32,24,128]{2,1,0:T(8,128)}, f32[18,128]{1,0:T(8,128)}) custom-call(f32[3,512]{1,0:T(4,128)} %get-tuple-element.21.x_ref, f32[3,512]{1,0:T(4,128)} %get-tuple-element.20.v_ref, f32[1,512]{1,0:T(1,128)} %bitcast.23, s32[1,768]{1,0:T(1,128)} %bitcast.18), custom_call_target="tpu_custom_call" | custom-call | tf_op jit(solution)/shard_map/spread/pallas_call | solution.py:275
  22.9 1.3 %slice_bitcast_fusion.1.x_ref = f32[18,128]{1,0:T(8,128)} fusion(f32[32,24,128]{2,1,0:T(8,128)} %get-tuple-element.10.x_ref.q_ref), kind=kLoop, calls=%fused_computation.1 | loop fusion | bytes 18432 | tf_op jit(solution)/shard_map/squeeze | solution.py:299
  24.2 22.7 %pairs.2.force_ref = f32[32,18,128]{2,1,0:T(8,128)} custom-call(s32[3,256]{1,0:T(4,128)} %bitcast.16, f32[32,24,128]{2,1,0:T(8,128)} %get-tuple-element.10.x_ref.q_ref, f32[32,24,128]{2,1,0:T(8,128)} %get-tuple-element.10.x_ref.q_ref), custom_call_target="tpu_custom_call" | custom-call | tf_op jit(solution)/shard_map/pairs/pallas_call | solution.py:298
  46.9 25.5 %advance.1 = (f32[32,24,128]{2,1,0:T(8,128)}, f32[18,128]{1,0:T(8,128)}) custom-call(f32[32,18,128]{2,1,0:T(8,128)} %pairs.2.force_ref, f32[18,128]{1,0:T(8,128)} %slice_bitcast_fusion.1.x_ref, f32[18,128]{1,0:T(8,128)} %get-tuple-element.11.vel_ref), custom_call_target="tpu_custom_call" | custom-call | tf_op jit(solution)/shard_map/advance/pallas_call | solution.py:301
  72.4 22.7 %pairs.3.force_ref = f32[32,18,128]{2,1,0:T(8,128)} custom-call(s32[3,256]{1,0:T(4,128)} %bitcast.17, f32[32,24,128]{2,1,0:T(8,128)} %get-tuple-element.12.x_ref, f32[32,24,128]{2,1,0:T(8,128)} %get-tuple-element.10.x_ref.q_ref), custom_call_target="tpu_custom_call" | custom-call | tf_op jit(solution)/shard_map/pairs/pallas_call | solution.py:298
  95.1 1.3 %slice_bitcast_fusion.x_ref = f32[18,128]{1,0:T(8,128)} fusion(f32[32,24,128]{2,1,0:T(8,128)} %get-tuple-element.12.x_ref), kind=kLoop, calls=%fused_computation | loop fusion | bytes 18432 | tf_op jit(solution)/shard_map/squeeze | solution.py:299
  96.4 14.6 %finish.1 = (f32[3,512]{1,0:T(4,128)}, f32[3,512]{1,0:T(4,128)}, f32[3,512]{1,0:T(4,128)}) custom-call(f32[32,18,128]{2,1,0:T(8,128)} %pairs.3.force_ref, f32[18,128]{1,0:T(8,128)} %slice_bitcast_fusion.x_ref, f32[18,128]{1,0:T(8,128)} %get-tuple-element.13.vel_ref, s32[1,768]{1,0:T(1,128)} %bitcast.19), custom_call_target="tpu_custom_call" | custom-call | tf_op jit(solution)/shard_map/finish/pallas_call | solution.py:312
  111.0 0.0 copy-start.2
  111.0 0.7 copy-done.2
  111.7 0.0 copy-start.1
  111.7 0.6 copy.8
  112.3 0.0 copy-start
  112.3 0.1 copy-done.1
  112.4 0.6 copy.9
  113.0 0.0 copy-done
  113.0 0.6 copy.10
Async XLA Ops:
  0.6 1.3 %copy-start.3 = (f32[3,1,1,1,512]{4,3,2,1,0:T(1,128)S(1)}, f32[3,1,1,1,512]{4,3,2,1,0:T(1,128)}, u32[]{:S(2)}) copy-start(f32[3,1,1,1,512]{4,3,2,1,0:T(1,128)} %param.6) | copy-start | bytes 18436
  0.6 1.3 %copy-start.4 = (f32[3,1,1,1,512]{4,3,2,1,0:T(1,128)S(1)}, f32[3,1,1,1,512]{4,3,2,1,0:T(1,128)}, u32[]{:S(2)}) copy-start(f32[3,1,1,1,512]{4,3,2,1,0:T(1,128)} %param.5) | copy-start | bytes 18436
  111.0 0.7 copy-start.2
  111.7 0.7 copy-start.1
  112.3 0.7 copy-start

commit v2 on v1

v2 whole, which is shorter than its diff:
```python
import functools

import jax
import jax.numpy as jnp
from jax import lax
from jax.experimental import pallas as pl
from jax.experimental.pallas import tpu as pltpu
from jax.sharding import PartitionSpec as P

CLUSTER = 128
STEPS = 2
TIME_STEP = 0.02
MESH = pl.DeviceIdType.MESH
AXES = ("gx", "gy", "gz")
VMEM = pl.BlockSpec(memory_space=pltpu.VMEM)
SMEM = pl.BlockSpec(memory_space=pltpu.SMEM)
UNROLL = 4


def split3(value):
    hi = value.astype(jnp.bfloat16)
    rest = value - hi.astype(jnp.float32)
    mid = rest.astype(jnp.bfloat16)
    lo = (rest - mid.astype(jnp.float32)).astype(jnp.bfloat16)
    return hi, mid, lo


class Zone:
    def __init__(self, sizes):
        self.sizes = sizes
        self.spans = tuple(min(5, n) for n in sizes)
        self.lows = tuple(-2 if n >= 5 else 0 for n in sizes)
        self.count = self.spans[0] * self.spans[1] * self.spans[2]
        own = tuple(-low for low in self.lows)
        self.own = (own[0] * self.spans[1] + own[1]) * self.spans[2] + own[2]

    def place(self, deltas):
        index = 0
        for delta, n, span in zip(deltas, self.sizes, self.spans):
            if n >= 5:
                here = delta + 2
            elif n in (1, 2, 4):
                here = (delta + 2 * n) & (n - 1)
            else:
                here = lax.rem(delta + 2 * n, n)
            index = index * span + here
        return index

    def peer(self, index, sign):
        parts = (
            index // (self.spans[1] * self.spans[2]),
            (index // self.spans[2]) % self.spans[1],
            index % self.spans[2],
        )
        out = []
        for axis, n, low, part in zip(AXES, self.sizes, self.lows, parts):
            out.append((lax.axis_index(axis) + sign * (part + low) + 2 * n) % n)
        return tuple(out)

    def others(self, body):
        def step(k, carry):
            body((self.own + 1 + k) % self.count)
            return carry

        lax.fori_loop(0, self.count - 1, step, 0)


def one_hot(atoms_ref, atom_count):
    slots = atoms_ref.shape[1]
    rows = lax.broadcasted_iota(jnp.int32, (atom_count, slots), 0)
    return jnp.where(rows == atoms_ref[...], 1.0, 0.0).astype(jnp.bfloat16)


def rows_where(count, index):
    rows = lax.broadcasted_iota(jnp.int32, (count, index.shape[1]), 0)
    return jnp.where(rows == index, 1.0, 0.0).astype(jnp.bfloat16)


def exact_dot(selector, values):
    return sum(
        jnp.dot(selector, piece, preferred_element_type=jnp.float32) for piece in split3(values)
    )


def side_by_side(ref):
    return jnp.concatenate([ref[c] for c in range(ref.shape[0])], axis=1)


def share(zone, src, dst_ref, send_sem, recv_sem):
    def copy(index):
        return pltpu.make_async_remote_copy(
            src_ref=src,
            dst_ref=dst_ref.at[index],
            send_sem=send_sem.at[index],
            recv_sem=recv_sem.at[index],
            device_id=zone.peer(index, -1),
            device_id_type=MESH,
        )

    zone.others(lambda index: copy(index).start())
    zone.others(lambda index: copy(index).wait())


def gathered_force(zone, force_ref, land_ref, send_sem, recv_sem):
    def copy(index):
        return pltpu.make_async_remote_copy(
            src_ref=force_ref.at[index],
            dst_ref=land_ref.at[index],
            send_sem=send_sem.at[index],
            recv_sem=recv_sem.at[index],
            device_id=zone.peer(index, 1),
            device_id_type=MESH,
        )

    zone.others(lambda index: copy(index).start())
    zone.others(lambda index: copy(index).wait())

    def add(k, total):
        return total + land_ref[(zone.own + 1 + k) % zone.count]

    return lax.fori_loop(0, zone.count - 1, add, force_ref[zone.own])


def weighted(coords, charge):
    charge = 0.125 * charge
    part = jnp.concatenate([charge * c for c in coords] + [charge], axis=0)
    pieces = [p.astype(jnp.float32) for p in split3(part)]
    stacked = jnp.concatenate(pieces + [jnp.zeros_like(part)], axis=0).astype(jnp.bfloat16)
    return jnp.concatenate([stacked, stacked], axis=1)


def folded(out):
    return out[0:4] + out[4:8] + out[8:12]


def shift_of(t):
    t25 = (t * 5243) >> 17
    t5 = (t * 205) >> 10
    return t25 - 2, t5 - 5 * t25 - 2, t - 5 * t5 - 2


def pair_forces(zone, clusters, pairs_ref, x_ref, q_ref, force_ref, left_ref, lw_ref,
                f_ref, right_sum_ref, left_sum_ref, zone_hot_ref, home_hot_ref):
    own = zone.own
    for k in range(clusters):
        coords = []
        for c in range(3):
            row = x_ref[own, pl.ds(c * clusters + k, 1), :]
            coords.append(row)
            left_ref[k, c] = jnp.transpose(jnp.broadcast_to(0.5 * row, (CLUSTER, CLUSTER)))
        lw_ref[k] = weighted(coords, q_ref[own, pl.ds(3 * clusters + k, 1), :])

    def right_side(p):
        j = pairs_ref[1, 0, p]
        deltas = shift_of(pairs_ref[2, 0, p])
        z = zone.place(deltas)
        coords = [
            x_ref[z, pl.ds(c * clusters + j, 1), :] + deltas[c].astype(jnp.float32)
            for c in range(3)
        ]
        return coords, q_ref[z, pl.ds(3 * clusters + j, 1), :]

    def geometry(b):
        for n in range(UNROLL):
            p = b * UNROLL + n
            coords, _ = right_side(p)
            i = pairs_ref[0, 0, p]
            r2 = None
            for c in range(3):
                d = left_ref[i, c] - 0.5 * coords[c]
                r2 = d * d if r2 is None else r2 + d * d
            g = jnp.maximum(1.0 - r2, 0.0)
            den = r2 + 0.125
            start = pl.reciprocal(den, approx=True)
            t = (g * start) * (2.0 - den * start)
            f = (g * t) * (t + 3.0)
            hi = f.astype(jnp.bfloat16)
            f_ref[n, 0] = hi
            f_ref[n, 1] = (f - hi.astype(jnp.float32)).astype(jnp.bfloat16)

    def sums(b):
        found = []
        for n in range(UNROLL):
            p = b * UNROLL + n
            hi, lo = f_ref[n, 0], f_ref[n, 1]
            coords, charge = right_side(p)
            left = lax.dot_general(
                weighted(coords, charge), jnp.concatenate([hi, lo], axis=1),
                (((1,), (1,)), ((), ())), preferred_element_type=jnp.float32,
            )
            right = jnp.dot(
                lw_ref[pairs_ref[0, 0, p]], jnp.concatenate([hi, lo], axis=0),
                preferred_element_type=jnp.float32,
            )
            found.append((p, coords, charge, left, right))
        return found

    def keep(found):
        for p, coords, charge, left, right in found:
            left = folded(left)
            right = folded(right)
            for c in range(4):
                left_sum_ref[c, pl.ds(p, 1), :] = left[c : c + 1]
            for c in range(3):
                right_sum_ref[c, pl.ds(p, 1), :] = charge * (
                    coords[c] * right[3:4] - right[c : c + 1]
                )

    blocks = pairs_ref.shape[2] // UNROLL
    geometry(0)

    def block(b, carry):
        found = sums(b - 1)
        geometry(b)
        keep(found)
        return carry

    lax.fori_loop(1, blocks, block, 0)
    keep(sums(blocks - 1))

    zone_out = exact_dot(zone_hot_ref[...], side_by_side(right_sum_ref))
    home_out = exact_dot(home_hot_ref[...], side_by_side(left_sum_ref))
    for z in range(zone.count):
        for c in range(3):
            force_ref[z, c * clusters : (c + 1) * clusters, :] = zone_out[
                z * 8 : z * 8 + clusters, c * CLUSTER : (c + 1) * CLUSTER
            ]
    for c in range(3):
        rows = slice(c * clusters, (c + 1) * clusters)
        total = home_out[0:clusters, 3 * CLUSTER :]
        moment = home_out[0:clusters, c * CLUSTER : (c + 1) * CLUSTER]
        charge = q_ref[own, 3 * clusters : 4 * clusters, :]
        force_ref[own, rows, :] += charge * (x_ref[own, rows, :] * total - moment)


def kernel(zone, pairs_ref, pairs_vec_ref, x_in, v_in, q_in, atoms_ref, x_out, v_out, f_out,
           zone0_ref, zone1_ref, vel_ref, pos_ref, force_ref, land_ref, slot_ref, left_ref, lw_ref, f_ref,
           right_sum_ref, left_sum_ref, zone_hot_ref, home_hot_ref, send_sem, recv_sem):
    atom_count = x_in.shape[2]
    slots = atoms_ref.shape[1]
    clusters = slots // CLUSTER
    rows = 3 * clusters
    own = zone.own
    barrier = pltpu.get_barrier_semaphore()
    zone.others(lambda index: pl.semaphore_signal(
        barrier, 1, device_id=zone.peer(index, 1), device_id_type=MESH))

    data = jnp.concatenate(
        [x_in[c] for c in range(3)] + [v_in[c] for c in range(3)]
        + [q_in[...], jnp.zeros((1, atom_count), jnp.float32)], axis=0
    )
    hi, mid, lo = split3(data)
    stacked = jnp.concatenate([hi, mid, lo, jnp.zeros_like(hi)], axis=0)
    out = jnp.dot(stacked, one_hot(atoms_ref, atom_count), preferred_element_type=jnp.float32)
    slot = out[0:8] + out[8:16] + out[16:24]
    for k in range(clusters):
        lanes = slice(k * CLUSTER, (k + 1) * CLUSTER)
        for c in range(3):
            zone0_ref[own, c * clusters + k, :] = slot[c, lanes]
            vel_ref[c * clusters + k, :] = slot[3 + c, lanes]
        zone0_ref[own, 3 * clusters + k, :] = slot[6, lanes]
    deltas = shift_of(pairs_vec_ref[2])
    zone_hot_ref[...] = rows_where(zone.count * 8, zone.place(deltas) * 8 + pairs_vec_ref[1])
    home_hot_ref[...] = rows_where(8, pairs_vec_ref[0])
    pl.semaphore_wait(barrier, zone.count - 1)
    share(zone, zone0_ref.at[own], zone0_ref, send_sem.at[0], recv_sem.at[0])

    for step in range(STEPS):
        x_ref = zone0_ref if step == 0 else zone1_ref.at[step - 1]
        pair_forces(zone, clusters, pairs_ref, x_ref, zone0_ref, force_ref, left_ref, lw_ref,
                    f_ref, right_sum_ref, left_sum_ref, zone_hot_ref, home_hot_ref)
        force = gathered_force(zone, force_ref, land_ref.at[step],
                               send_sem.at[2 * step + 1], recv_sem.at[2 * step + 1])
        velocity = vel_ref[...] + TIME_STEP * force
        coords = x_ref[own, 0:rows, :] + TIME_STEP * velocity
        if step < STEPS - 1:
            vel_ref[...] = velocity
            zone1_ref[step, own] = coords
            share(zone, zone1_ref.at[step, own], zone1_ref.at[step],
                  send_sem.at[2 * step + 2], recv_sem.at[2 * step + 2])

    slot_ref[...] = jnp.zeros_like(slot_ref)
    for k in range(clusters):
        lanes = slice(k * CLUSTER, (k + 1) * CLUSTER)
        for c in range(3):
            r = c * clusters + k
            slot_ref[pl.ds(c, 1), lanes] = coords[r : r + 1]
            slot_ref[pl.ds(3 + c, 1), lanes] = velocity[r : r + 1]
            slot_ref[pl.ds(6 + c, 1), lanes] = force[r : r + 1]
    stacked = jnp.concatenate(split3(slot_ref[...]), axis=0)
    out = lax.dot_general(
        stacked, one_hot(atoms_ref, atom_count), (((1,), (1,)), ((), ())),
        preferred_element_type=jnp.float32,
    )
    atom = out[0:16] + out[16:32] + out[32:48]
    for c in range(3):
        x_out[c] = atom[c : c + 1]
        v_out[c] = atom[3 + c : 4 + c]
        f_out[c] = atom[6 + c : 7 + c]


def shards(sizes, positions, velocities, charges, cluster_atoms, pair_list):
    zone = Zone(sizes)
    atom_count = positions.shape[-1]
    slots = cluster_atoms.shape[-1]
    pair_count = pair_list.shape[-1]
    clusters = slots // CLUSTER
    rows = 3 * clusters
    f32, bf16 = jnp.float32, jnp.bfloat16
    x = positions.reshape(3, 1, atom_count)
    v = velocities.reshape(3, 1, atom_count)
    q = charges.reshape(1, atom_count)
    atoms = cluster_atoms.reshape(1, slots)
    pairs = pair_list.reshape(3, 1, pair_count)
    shape = jax.ShapeDtypeStruct((3, 1, atom_count), f32)
    outs = pl.pallas_call(
        functools.partial(kernel, zone),
        out_shape=(shape, shape, shape),
        in_specs=[SMEM] + [VMEM] * 5,
        out_specs=(VMEM, VMEM, VMEM),
        scratch_shapes=[
            pltpu.VMEM((zone.count, 4 * clusters, CLUSTER), f32),
            pltpu.VMEM((STEPS - 1, zone.count, rows, CLUSTER), f32),
            pltpu.VMEM((rows, CLUSTER), f32),
            pltpu.VMEM((rows, CLUSTER), f32),
            pltpu.VMEM((zone.count, rows, CLUSTER), f32),
            pltpu.VMEM((STEPS, zone.count, rows, CLUSTER), f32),
            pltpu.VMEM((16, slots), f32),
            pltpu.VMEM((clusters, 3, CLUSTER, CLUSTER), f32),
            pltpu.VMEM((clusters, 16, 2 * CLUSTER), bf16),
            pltpu.VMEM((UNROLL, 2, CLUSTER, CLUSTER), bf16),
            pltpu.VMEM((3, pair_count, CLUSTER), f32),
            pltpu.VMEM((4, pair_count, CLUSTER), f32),
            pltpu.VMEM((zone.count * 8, pair_count), bf16),
            pltpu.VMEM((8, pair_count), bf16),
            pltpu.SemaphoreType.DMA((2 * STEPS, zone.count)),
            pltpu.SemaphoreType.DMA((2 * STEPS, zone.count)),
        ],
        compiler_params=pltpu.CompilerParams(collective_id=0, has_side_effects=True),
        name="leapfrog",
    )(pairs, pairs, x, v, q, atoms)
    return tuple(out.reshape(positions.shape) for out in outs)


def solution(mesh):
    spec3 = P(None, "gx", "gy", "gz", None)
    spec1 = P("gx", "gy", "gz", None)
    sizes = tuple(mesh.shape[axis] for axis in AXES)
    return jax.shard_map(
        functools.partial(shards, sizes),
        mesh=mesh,
        in_specs=(spec3, spec3, spec1, spec1, spec3),
        out_specs=(spec3, spec3, spec3),
        check_vma=False,
    )
```

time: 114 us -> 100 us (0.88)
  Pallas kernels: 106 us -> 96.4 us
  local copies, waits for them, and re-layouts: 7.1 us -> 2.67 us
    pallas_call x5 -> x1, Pallas kernels: 106 us -> 96.4 us  [shards(): pl.pallas_call(functools.partial(kernel, zone), out_shape=(shape, shape,...]
    squeeze x2 -> x0, local copies, waits for them, and re-layouts: 2.61 us -> none  [shards(): own_x = zone_x[zone.own, :rows]]
    unnamed x15 -> x9, local copies, waits for them, and re-layouts: 4.49 us -> 2.67 us
where the time goes in v2:
time: 100 us; the launch traced here: 99.7 us
  Pallas kernels  96.4 us (96%)
  local copies, waits for them, and re-layouts  2.67 us (3%)
    pallas_call x1, Pallas kernels, shards(): pl.pallas_call(functools.partial(kernel, zone), out_shape=(shape, shape,...  96.4 us
    unnamed x9, local copies, waits for them, and re-layouts  2.67 us

profile of v2, /device:TPU:0, one launch (start us, length us, event | category | flops | bytes accessed | tf_op | source)
XLA Modules:
  0.0 99.7 jit_solution(14284661096908389493)
XLA Ops:
  0.6 96.4 %leapfrog.1 = (f32[3,1,512]{2,1,0:T(1,128)}, f32[3,1,512]{2,1,0:T(1,128)}, f32[3,1,512]{2,1,0:T(1,128)}) custom-call(s32[3,1,256]{2,1,0:T(1,128)} %bitcast.14, s32[3,1,256]{2,1,0:T(1,128)} %bitcast.15, f32[3,1,512]{2,1,0:T(1,128)} %bitcast.19, f32[3,1,512]{2,1,0:T(1,128)} %bitcast.20, f32[1,512]{1,0:T(1,128)} %bitcast.22, s32[1,768]{1,0:T(1,128)} %bitcast.21), custom_call_target="tpu_custom_call" | custom-call | tf_op jit(solution)/shard_map/leapfrog/pallas_call | solution.py:316
  97.0 0.0 copy-start.2
  97.0 0.7 copy-done.2
  97.7 0.0 copy-start.1
  97.7 0.6 copy.14
  98.3 0.1 copy-done.1
  98.4 0.0 copy-start
  98.4 0.6 copy.15
  99.0 0.1 copy-done
  99.1 0.6 copy.16
Async XLA Ops:
  97.0 0.7 copy-start.2
  97.7 0.7 copy-start.1
  98.4 0.7 copy-start

commit v3 on v2

--- a/solution.py
+++ b/solution.py
@@ -14,7 +14,7 @@
 AXES = ("gx", "gy", "gz")
 VMEM = pl.BlockSpec(memory_space=pltpu.VMEM)
 SMEM = pl.BlockSpec(memory_space=pltpu.SMEM)
-UNROLL = 4
+UNROLL = 16
 
 
 def split3(value):
@@ -32,6 +32,8 @@
         self.lows = tuple(-2 if n >= 5 else 0 for n in sizes)
         self.count = self.spans[0] * self.spans[1] * self.spans[2]
         own = tuple(-low for low in self.lows)
+        self.paired = max(sizes) <= 4 and sizes[0] % 2 == 0
+        self.plane = self.spans[1] * self.spans[2]
         self.own = (own[0] * self.spans[1] + own[1]) * self.spans[2] + own[2]
 
     def place(self, deltas):
@@ -57,6 +59,24 @@
             out.append((lax.axis_index(axis) + sign * (part + low) + 2 * n) % n)
         return tuple(out)
 
+    def turn(self):
+        return 1 - 2 * (lax.axis_index(AXES[0]) % 2)
+
+    def partner(self):
+        return (lax.axis_index(AXES[0]) + self.turn(),) + tuple(
+            lax.axis_index(axis) for axis in AXES[1:]
+        )
+
+    def seen_by_partner(self, index):
+        return (index - self.turn() * self.plane + self.count) % self.count
+
+    def alike(self, body):
+        def step(k, carry):
+            body((k // self.plane) * 2 * self.plane + k % self.plane)
+            return carry
+
+        lax.fori_loop(1, self.count // 2, step, 0)
+
     def others(self, body):
         def step(k, carry):
             body((self.own + 1 + k) % self.count)
@@ -97,8 +117,47 @@
             device_id_type=MESH,
         )
 
-    zone.others(lambda index: copy(index).start())
-    zone.others(lambda index: copy(index).wait())
+    if not zone.paired:
+        zone.others(lambda index: copy(index).start())
+        zone.others(lambda index: copy(index).wait())
+        return
+
+    def relay(index, block):
+        place = zone.seen_by_partner(index)
+        return pltpu.make_async_remote_copy(
+            src_ref=block,
+            dst_ref=dst_ref.at[place],
+            send_sem=send_sem.at[(index + zone.plane) % zone.count],
+            recv_sem=recv_sem.at[place],
+            device_id=zone.partner(),
+            device_id_type=MESH,
+        )
+
+    zone.alike(lambda index: copy(index).start())
+    relay(zone.own, src).start()
+
+    def pass_on(index):
+        copy(index).wait_recv()
+        relay(index, dst_ref.at[index]).start()
+
+    zone.alike(pass_on)
+    zone.alike(lambda index: copy(index).wait_send())
+
+    def settle(k, carry):
+        index = (k // zone.plane) * 2 * zone.plane + k % zone.plane
+        relay(index, src).wait_send()
+        arrived = pltpu.make_async_remote_copy(
+            src_ref=src,
+            dst_ref=dst_ref.at[index + zone.plane],
+            send_sem=send_sem.at[index + zone.plane],
+            recv_sem=recv_sem.at[index + zone.plane],
+            device_id=zone.partner(),
+            device_id_type=MESH,
+        )
+        arrived.wait_recv()
+        return carry
+
+    lax.fori_loop(0, zone.count // 2, settle, 0)
 
 
 def gathered_force(zone, force_ref, land_ref, send_sem, recv_sem):
@@ -112,13 +171,54 @@
             device_id_type=MESH,
         )
 
-    zone.others(lambda index: copy(index).start())
-    zone.others(lambda index: copy(index).wait())
+    if not zone.paired:
+        zone.others(lambda index: copy(index).start())
+        zone.others(lambda index: copy(index).wait())
+
+        def add(k, total):
+            return total + land_ref[(zone.own + 1 + k) % zone.count]
+
+        return lax.fori_loop(0, zone.count - 1, add, force_ref[zone.own])
+
+    def handed(part):
+        odd = (2 * part + 1) * zone.plane
+        return pltpu.make_async_remote_copy(
+            src_ref=force_ref.at[pl.ds(odd, zone.plane)],
+            dst_ref=land_ref.at[pl.ds(zone.count + zone.seen_by_partner(odd), zone.plane)],
+            send_sem=send_sem.at[odd],
+            recv_sem=recv_sem.at[zone.count + zone.seen_by_partner(odd)],
+            device_id=zone.partner(),
+            device_id_type=MESH,
+        )
+
+    def taken(part):
+        even = 2 * part * zone.plane
+        return pltpu.make_async_remote_copy(
+            src_ref=force_ref.at[pl.ds(even, zone.plane)],
+            dst_ref=land_ref.at[pl.ds(zone.count + even, zone.plane)],
+            send_sem=send_sem.at[even],
+            recv_sem=recv_sem.at[zone.count + even],
+            device_id=zone.partner(),
+            device_id_type=MESH,
+        )
+
+    parts = zone.count // (2 * zone.plane)
+    for part in range(parts):
+        handed(part).start()
+    for part in range(parts):
+        taken(part).wait_recv()
+        even = 2 * part * zone.plane
+        for k in range(zone.plane):
+            force_ref[even + k] += land_ref[zone.count + even + k]
+    zone.alike(lambda index: copy(index).start())
+    for part in range(parts):
+        handed(part).wait_send()
+    zone.alike(lambda index: copy(index).wait())
 
     def add(k, total):
-        return total + land_ref[(zone.own + 1 + k) % zone.count]
-
-    return lax.fori_loop(0, zone.count - 1, add, force_ref[zone.own])
+        return total + land_ref[(k // zone.plane) * 2 * zone.plane + k % zone.plane]
+
+    return lax.fori_loop(1, zone.count // 2, add, force_ref[zone.own])
 
 
 def weighted(coords, charge):
@@ -324,7 +424,7 @@
             pltpu.VMEM((rows, CLUSTER), f32),
             pltpu.VMEM((rows, CLUSTER), f32),
             pltpu.VMEM((zone.count, rows, CLUSTER), f32),
-            pltpu.VMEM((STEPS, zone.count, rows, CLUSTER), f32),
+            pltpu.VMEM((STEPS, 2 * zone.count, rows, CLUSTER), f32),
             pltpu.VMEM((16, slots), f32),
             pltpu.VMEM((clusters, 3, CLUSTER, CLUSTER), f32),
             pltpu.VMEM((clusters, 16, 2 * CLUSTER), bf16),
@@ -333,8 +433,8 @@
             pltpu.VMEM((4, pair_count, CLUSTER), f32),
             pltpu.VMEM((zone.count * 8, pair_count), bf16),
             pltpu.VMEM((8, pair_count), bf16),
-            pltpu.SemaphoreType.DMA((2 * STEPS, zone.count)),
-            pltpu.SemaphoreType.DMA((2 * STEPS, zone.count)),
+            pltpu.SemaphoreType.DMA((2 * STEPS, 2 * zone.count)),
+            pltpu.SemaphoreType.DMA((2 * STEPS, 2 * zone.count)),
         ],
         compiler_params=pltpu.CompilerParams(collective_id=0, has_side_effects=True),
         name="leapfrog",

time: 100 us -> 82.2 us (0.82)
  Pallas kernels: 96.4 us -> 78.6 us
    pallas_call x1, Pallas kernels: 96.4 us -> 78.6 us  [shards(): pl.pallas_call(functools.partial(kernel, zone), out_shape=(shape, shape,...]
where the time goes in v3:
time: 82.2 us; the launch traced here: 81.9 us
  Pallas kernels  78.6 us (96%)
  local copies, waits for them, and re-layouts  2.67 us (3%)
    pallas_call x1, Pallas kernels, shards(): pl.pallas_call(functools.partial(kernel, zone), out_shape=(shape, shape,...  78.6 us
    unnamed x9, local copies, waits for them, and re-layouts  2.67 us

profile of v3, /device:TPU:0, one launch (start us, length us, event | category | flops | bytes accessed | tf_op | source)
XLA Modules:
  0.0 81.9 jit_solution(15174590580951000492)
XLA Ops:
  0.6 78.6 %leapfrog.1 = (f32[3,1,512]{2,1,0:T(1,128)}, f32[3,1,512]{2,1,0:T(1,128)}, f32[3,1,512]{2,1,0:T(1,128)}) custom-call(s32[3,1,256]{2,1,0:T(1,128)} %bitcast.14, s32[3,1,256]{2,1,0:T(1,128)} %bitcast.15, f32[3,1,512]{2,1,0:T(1,128)} %bitcast.19, f32[3,1,512]{2,1,0:T(1,128)} %bitcast.20, f32[1,512]{1,0:T(1,128)} %bitcast.22, s32[1,768]{1,0:T(1,128)} %bitcast.21), custom_call_target="tpu_custom_call" | custom-call | tf_op jit(solution)/shard_map/leapfrog/pallas_call | solution.py:416
  79.2 0.0 copy-start.2
  79.2 0.7 copy-done.2
  79.9 0.0 copy-start.1
  79.9 0.6 copy.14
  80.5 0.1 copy-done.1
  80.6 0.0 copy-start
  80.6 0.6 copy.15
  81.2 0.1 copy-done
  81.3 0.6 copy.16
Async XLA Ops:
  79.2 0.7 copy-start.2
  79.9 0.7 copy-start.1
  80.6 0.7 copy-start

commit v4 on v3

--- a/solution.py
+++ b/solution.py
@@ -14,7 +14,7 @@
 AXES = ("gx", "gy", "gz")
 VMEM = pl.BlockSpec(memory_space=pltpu.VMEM)
 SMEM = pl.BlockSpec(memory_space=pltpu.SMEM)
-UNROLL = 16
+UNROLL = 32
 
 
 def split3(value):
@@ -260,8 +260,8 @@
         ]
         return coords, q_ref[z, pl.ds(3 * clusters + j, 1), :]
 
-    def geometry(b):
-        for n in range(UNROLL):
+    def geometry(b, which=range(UNROLL)):
+        for n in which:
             p = b * UNROLL + n
             coords, _ = right_side(p)
             i = pairs_ref[0, 0, p]
@@ -278,9 +278,9 @@
             f_ref[n, 0] = hi
             f_ref[n, 1] = (f - hi.astype(jnp.float32)).astype(jnp.bfloat16)
 
-    def sums(b):
+    def sums(b, which=range(UNROLL)):
         found = []
-        for n in range(UNROLL):
+        for n in which:
             p = b * UNROLL + n
             hi, lo = f_ref[n, 0], f_ref[n, 1]
             coords, charge = right_side(p)
@@ -310,9 +310,13 @@
     geometry(0)
 
     def block(b, carry):
-        found = sums(b - 1)
-        geometry(b)
-        keep(found)
+        found = []
+        for n in range(UNROLL):
+            found += sums(b - 1, [n])
+            geometry(b, [n])
+            if n > 1:
+                keep(found[n - 2 : n - 1])
+        keep(found[-2:])
         return carry
 
     lax.fori_loop(1, blocks, block, 0)

time: 82.2 us -> 81 us (0.985)
  Pallas kernels: 78.6 us -> 77.3 us
    pallas_call x1, Pallas kernels: 78.6 us -> 77.3 us  [shards(): pl.pallas_call(functools.partial(kernel, zone), out_shape=(shape, shape,...]
where the time goes in v4:
time: 81 us; the launch traced here: 80.7 us
  Pallas kernels  77.3 us (95%)
  local copies, waits for them, and re-layouts  2.67 us (3%)
    pallas_call x1, Pallas kernels, shards(): pl.pallas_call(functools.partial(kernel, zone), out_shape=(shape, shape,...  77.3 us
    unnamed x9, local copies, waits for them, and re-layouts  2.67 us

profile of v4, /device:TPU:0, one launch (start us, length us, event | category | flops | bytes accessed | tf_op | source)
XLA Modules:
  0.0 80.7 jit_solution(4855087168671695760)
XLA Ops:
  0.6 77.3 %leapfrog.1 = (f32[3,1,512]{2,1,0:T(1,128)}, f32[3,1,512]{2,1,0:T(1,128)}, f32[3,1,512]{2,1,0:T(1,128)}) custom-call(s32[3,1,256]{2,1,0:T(1,128)} %bitcast.14, s32[3,1,256]{2,1,0:T(1,128)} %bitcast.15, f32[3,1,512]{2,1,0:T(1,128)} %bitcast.19, f32[3,1,512]{2,1,0:T(1,128)} %bitcast.20, f32[1,512]{1,0:T(1,128)} %bitcast.22, s32[1,768]{1,0:T(1,128)} %bitcast.21), custom_call_target="tpu_custom_call" | custom-call | tf_op jit(solution)/shard_map/leapfrog/pallas_call | solution.py:420
  78.0 0.0 copy-start.2
  78.0 0.7 copy-done.2
  78.7 0.0 copy-start.1
  78.7 0.6 copy.14
  79.3 0.1 copy-done.1
  79.4 0.0 copy-start
  79.4 0.6 copy.15
  80.0 0.1 copy-done
  80.1 0.6 copy.16
Async XLA Ops:
  78.0 0.7 copy-start.2
  78.7 0.7 copy-start.1
  79.4 0.7 copy-start
